TPU v7x, 32 devices: a whole 2x2x4 slice. The times are simulated.
32 devices in a mesh: row: 4 (over y, x), col: 8 (over z, core).
Axes of the slice: x: 2, y: 2, z: 4, core: 2. Of those that a mesh axis runs over, the one named last changes fastest.
Arguments:
- model_gradient: float32 [3, 512, 512, 256], P(None, 'row', 'col'), may hold values from -6 to 6
- filter_x: float32 [512, 512], replicated, may hold values from 0 to 1, as said below
- filter_y: float32 [512, 512], replicated, may hold values from 0 to 1, as said below
- filter_z: float32 [256, 256], replicated, may hold values from 0 to 1, as said below
- depth_scale: float32 [3, 256], replicated, may hold values from 0.3 to 3
Outputs:
- smoothed: float32 [3, 512, 512, 256], P(None, 'row', 'col')
Inputs may be any that keep to these rules, and one draw needn't show every extreme that they name: `filter_x`: each row is a nonnegative smoothing kernel of its own width plus one half on the diagonal; rows sum to one. `filter_y`: each row is a nonnegative smoothing kernel of its own width plus one half on the diagonal; rows sum to one. `filter_z`: each row is a nonnegative smoothing kernel of its own width plus one half on the diagonal; rows sum to one.
All inputs are finite; a program needn't handle non-finite values.
Results may differ from a plain program's by a relative error of at most 0.0001.
Values sent between devices are 32-bit elements; how exact they have to be, the bound alone decides.
A program may use at most 192 MiB of HBM per device.

v0:
```python
import jax
import jax.numpy as jnp
from jax import lax
from jax.sharding import PartitionSpec as P


def plane_filter(incoming_part, filter_x, filter_y, rows, cols):
    highest_accuracy = lax.Precision.HIGHEST
    params, xloc, yloc = (incoming_part.shape[0], incoming_part.shape[1], incoming_part.shape[2])
    matrix_x = filter_x.reshape(rows, xloc, rows, xloc)
    lateral_y_matrix = filter_y.reshape(cols, yloc, cols, yloc)
    partial_value = jnp.einsum(
        "ABRa,pabRSz->ABpbSz", matrix_x, incoming_part, precision=highest_accuracy
    )
    return jnp.einsum(
        "CDSb,ABpbSz->ACpBDz", lateral_y_matrix, partial_value, precision=highest_accuracy
    )


def shards(model_gradient, filter_x, filter_y, filter_z, depth_scale):
    highest_accuracy = lax.Precision.HIGHEST
    rows = lax.axis_size("row")
    cols = lax.axis_size("col")
    params, xloc, yloc, depth = model_gradient.shape
    scaled_filter = depth_scale[:, :, None] * filter_z[None, :, :]
    column_first = jnp.einsum(
        "pkz,pabz->pabk", scaled_filter, model_gradient, precision=highest_accuracy
    )
    depth_block = depth // (rows * cols)
    outgoing = column_first.reshape(params, xloc, yloc, rows * cols, depth_block)
    incoming_part = lax.all_to_all(
        outgoing, ("row", "col"), split_axis=3, concat_axis=3, tiled=True
    )
    incoming_part = incoming_part.reshape(params, xloc, yloc, rows, cols, depth_block)
    planes = plane_filter(incoming_part, filter_x, filter_y, rows, cols)
    planes = planes.reshape(rows * cols, params, xloc, yloc, depth_block)
    result = lax.all_to_all(planes, ("row", "col"), split_axis=0, concat_axis=4, tiled=True)
    return result.reshape(params, xloc, yloc, depth)


def solution(mesh):
    return jax.shard_map(
        shards,
        mesh=mesh,
        in_specs=(P(None, "row", "col", None), P(), P(), P(), P()),
        out_specs=P(None, "row", "col", None),
        check_vma=False,
    )
```

profile of v0, /device:TPU:0, one launch (start us, length us, event | category | flops | bytes accessed | tf_op | source)
XLA Modules:
  0.0 1324.2 jit_solution(16032111369222720225)
XLA Ops:
  0.0 44.2 %fusion.7 = f32[3,128,64,32,8]{1,4,3,2,0:T(8,128)} fusion(f32[3,128,64,256]{3,2,1,0:T(8,128)} %param.5, f32[256,256]{1,0:T(8,128)} %param.8, f32[3,256]{1,0:T(4,128)} %param.9), kind=kOutput, calls=%fused_computation.8 | convolution fusion | flops 19327549440 | bytes 50596864 | tf_op jit(solution)/shard_map/pkz,pabz->pabk/dot_general | solution.py:26
  44.2 17.2 %copy.21 = f32[3,128,64,32,8]{1,4,2,0,3:T(8,128)} copy(f32[3,128,64,32,8]{1,4,3,2,0:T(8,128)} %fusion.7) | data formatting | bytes 50331648 | tf_op jit(solution)/shard_map/reshape | solution.py:30
  61.4 0.0 copy-start
  61.4 7.6 all-to-all-start
  69.0 0.0 copy-done
  69.0 0.4 reshape.23
  69.4 1.6 reshape.24
  71.0 542.2 %all-to-all-done = f32[3,128,64,32,8]{1,4,2,0,3:T(8,128)} async-done(((f32[3,128,64,32,8]{1,4,2,0,3:T(8,128)}), f32[3,128,64,32,8]{1,4,2,0,3:T(8,128)}, u32[]{:S(2)}, u32[]{:S(2)}) %all-to-all-start) | async-done | bytes 25165856 | tf_op jit(solution)/shard_map/all_to_all | solution.py:31
  613.2 49.8 %fusion.2 = f32[3,64,8,8,4,128,1]{5,1,6,2,3,0,4:T(8,128)S(1)} fusion(f32[3,128,64,4,8,8]{1,5,2,0,4,3:T(8,128)} %bitcast.4, f32[4,128,4,128,1,1,1]{3,2,1,0,6,5,4:T(4,128)S(1)} %bitcast.41), kind=kOutput, calls=%fused_computation.2 | convolution fusion | flops 38654705664 | bytes 51380224 | tf_op jit(solution)/shard_map/ABRa,pabRSz->ABpbSz/dot_general | solution.py:12
  663.0 45.9 %fusion.10 = f32[4,8,3,128,64,8]{3,4,1,5,2,0:T(8,128)} fusion(f32[3,64,8,8,4,128,1]{5,1,6,2,3,0,4:T(8,128)S(1)} %fusion.2, f32[8,64,8,64,1,1,1]{3,2,1,0,6,5,4:T(8,128)S(1)} %bitcast.42), kind=kOutput, calls=%fused_computation.9 | convolution fusion | flops 38654705664 | bytes 51380224 | tf_op jit(solution)/shard_map/CDSb,ABpbSz->ACpBDz/dot_general | solution.py:15
  708.9 26.2 %copy.26 = f32[4,8,3,128,64,8]{3,5,4,2,1,0:T(8,128)S(1)} copy(f32[4,8,3,128,64,8]{3,4,1,5,2,0:T(8,128)} %fusion.10) | data formatting | bytes 50331648 | tf_op jit(solution)/shard_map/CDSb,ABpbSz->ACpBDz/transpose | solution.py:15
  735.1 547.0 %all_to_all.20 = f32[32,3,128,64,8]{2,4,3,1,0:T(8,128)} all-to-all(f32[32,3,128,64,8]{2,4,3,1,0:T(8,128)S(1)} %bitcast.40), channel_id=1, replica_groups=mesh['row'=4,'col'=8] {'row','col'}, dimensions={0} | all-to-all | bytes 50331648 | tf_op jit(solution)/shard_map/all_to_all | solution.py:37
  1282.1 17.4 %copy_bitcast_fusion = f32[3,128,64,256]{1,3,2,0:T(8,128)} fusion(f32[32,3,128,64,8]{2,4,3,1,0:T(8,128)} %all_to_all.20), kind=kLoop, calls=%fused_computation.5 | loop fusion | bytes 50331648 | tf_op jit(solution)/shard_map/reshape | solution.py:38
  1299.5 24.7 %copy.28 = f32[3,128,64,256]{3,2,1,0:T(8,128)} copy(f32[3,128,64,256]{1,3,2,0:T(8,128)} %copy_bitcast_fusion) | data formatting | bytes 50331648 | tf_op jit(solution)/shard_map/reshape | solution.py:38
Async XLA Ops:
  61.4 7.6 copy-start
  61.4 551.8 %all-to-all-start = ((f32[3,128,64,32,8]{1,4,2,0,3:T(8,128)}), f32[3,128,64,32,8]{1,4,2,0,3:T(8,128)}, u32[]{:S(2)}, u32[]{:S(2)}) async-start(f32[3,128,64,32,8]{1,4,2,0,3:T(8,128)} %copy.21), calls=%async_computation | async-start | bytes 50331648 | tf_op jit(solution)/shard_map/all_to_all | solution.py:31
where the time goes:
time: 1320 us
  blocking collectives  547 us (41%)
  waiting for transfers between devices  542 us (41%)
  matrix products  140 us (11%)
  local copies, waits for them, and re-layouts  87.5 us (7%)
    all_to_all x1, blocking collectives, shards(): lax.all_to_all(planes, ('row', 'col'), split_axis=0, concat_axis=4, tiled...  547 us
    all_to_all x1, waiting for transfers between devices, shards(): lax.all_to_all(outgoing, ('row', 'col'), split_axis=3, concat_axis=3, til...  542 us
    dot_general x1, matrix products, plane_filter(): jnp.einsum('ABRa,pabRSz->ABpbSz', matrix_x, incoming_part, precision=high...  49.8 us
    dot_general x1, matrix products, plane_filter(): jnp.einsum('CDSb,ABpbSz->ACpBDz', lateral_y_matrix, partial_value, precis...  45.9 us
    dot_general x1, matrix products, shards(): jnp.einsum('pkz,pabz->pabk', scaled_filter, model_gradient, precision=hig...  44.2 us
    reshape x2, local copies, waits for them, and re-layouts, shards(): return result.reshape(params, xloc, yloc, depth)  42.1 us
  transfers between devices with their start and end apart: 1, of which 1 were waited for; matrix products, arithmetic and copies ran while one was open for 0% of the time, Pallas kernels for 0%

commit v1 on v0

v1 whole, which is shorter than its diff:
```python
import jax
import jax.numpy as jnp
from jax import lax
from jax.experimental import pallas as pl
from jax.experimental.pallas import tpu as pltpu
from jax.sharding import PartitionSpec as P

ACCURACY = lax.Precision.HIGH
AXES = ("row", "col")
LAST = (((1,), (1,)), ((), ()))
INNER = (((1,), (0,)), ((), ()))


def split_outside(value):
    high = lax.reduce_precision(value, 8, 7)
    return high.astype(jnp.bfloat16), (value - high).astype(jnp.bfloat16)


def split(value):
    high = value.astype(jnp.bfloat16)
    return high, (value - high.astype(jnp.float32)).astype(jnp.bfloat16)


def dot3(left, right, dims):
    def one(a, b):
        return lax.dot_general(a, b, dims, preferred_element_type=jnp.float32)

    return one(left[0], right[0]) + (one(left[0], right[1]) + one(left[1], right[0]))


def cost(flops, count):
    return pl.CostEstimate(flops=flops, bytes_accessed=count, transcendentals=0)


def depth_kernel(high_ref, low_ref, field_ref, out_ref):
    _, xloc, tile, depth = field_ref.shape
    parts, _, block, _ = out_ref.shape
    filters = (high_ref[0], low_ref[0])
    for b in range(tile):
        piece = split(field_ref[0, :, b, :])
        column = dot3(filters, piece, LAST)
        out_ref[:, b] = column.reshape(parts, block, xloc)


def depth_pass(index, high, low, field, parts, tile):
    _, xloc, yloc, depth = field.shape
    block = depth // parts
    return pl.pallas_call(
        depth_kernel,
        grid=(yloc // tile,),
        in_specs=[
            pl.BlockSpec((1, depth, depth), lambda j: (index, 0, 0)),
            pl.BlockSpec((1, depth, depth), lambda j: (index, 0, 0)),
            pl.BlockSpec((1, xloc, tile, depth), lambda j: (index, 0, j, 0)),
        ],
        out_specs=pl.BlockSpec((parts, tile, block, xloc), lambda j: (0, j, 0, 0)),
        out_shape=jax.ShapeDtypeStruct((parts, yloc, block, xloc), jnp.float32),
        cost_estimate=cost(6 * xloc * yloc * depth * depth, 8 * xloc * yloc * depth),
    )(high, low, field)


def first_kernel(high_ref, low_ref, in_ref, out_ref):
    rows, _, yloc, block, xloc = in_ref.shape
    flat = [in_ref[r, 0].reshape(yloc * block, xloc) for r in range(rows)]
    piece = split(jnp.concatenate(flat, axis=1))
    for r in range(rows):
        part = pl.ds(r * xloc, xloc)
        value = dot3(piece, (high_ref[part, :], low_ref[part, :]), LAST)
        out_ref[r, 0] = value.reshape(yloc, block, xloc)


def first_pass(high, low, field):
    rows, cols, yloc, block, xloc = field.shape
    size = rows * xloc
    spec = pl.BlockSpec((rows, 1, yloc, block, xloc), lambda s: (0, s, 0, 0, 0))
    whole = pl.BlockSpec((size, size), lambda s: (0, 0))
    return pl.pallas_call(
        first_kernel,
        grid=(cols,),
        in_specs=[whole, whole, spec],
        out_specs=spec,
        out_shape=jax.ShapeDtypeStruct(field.shape, jnp.float32),
        cost_estimate=cost(6 * size * field.size, 8 * field.size),
    )(high, low, field)


def second_kernel(high_ref, low_ref, in_ref, out_ref):
    _, cols, yloc, block, xloc = in_ref.shape
    size = cols * yloc
    filters = (high_ref[...], low_ref[...])
    for k in range(0, block, 2):
        pair = [in_ref[0, :, :, k + n, :].reshape(size, xloc) for n in range(2)]
        value = dot3(filters, split(jnp.concatenate(pair, axis=1)), INNER)
        for n in range(2):
            part = value[:, n * xloc : (n + 1) * xloc]
            out_ref[0, :, :, k + n, :] = part.reshape(cols, yloc, xloc)


def second_pass(high, low, field):
    rows, cols, yloc, block, xloc = field.shape
    size = cols * yloc
    spec = pl.BlockSpec((1, cols, yloc, block, xloc), lambda r: (r, 0, 0, 0, 0))
    whole = pl.BlockSpec((size, size), lambda r: (0, 0))
    return pl.pallas_call(
        second_kernel,
        grid=(rows,),
        in_specs=[whole, whole, spec],
        out_specs=spec,
        out_shape=jax.ShapeDtypeStruct(field.shape, jnp.float32),
        cost_estimate=cost(6 * size * field.size, 8 * field.size),
    )(high, low, field)


def place_kernel(in_ref, *refs):
    out_ref = refs[-1]
    parts, tile, block, xloc = in_ref.shape
    for j in range(tile):
        plane = in_ref[:, j].reshape(parts * block, xloc)
        out_ref[0, :, j, :] = plane.T


def place(index, params, field, output, tile):
    parts, yloc, block, xloc = field.shape
    depth = parts * block
    given = [] if output is None else [output]
    return pl.pallas_call(
        place_kernel,
        grid=(yloc // tile,),
        in_specs=[pl.BlockSpec((parts, tile, block, xloc), lambda j: (0, j, 0, 0))]
        + [pl.BlockSpec(memory_space=pl.ANY) for _ in given],
        out_specs=pl.BlockSpec((1, xloc, tile, depth), lambda j: (index, 0, j, 0)),
        out_shape=jax.ShapeDtypeStruct((params, xloc, yloc, depth), jnp.float32),
        input_output_aliases={1: 0} if given else {},
        cost_estimate=cost(0, 8 * field.size),
    )(field, *given)


def kernel_shards(model_gradient, filter_x, filter_y, filter_z, depth_scale):
    rows, cols = lax.axis_size("row"), lax.axis_size("col")
    params, xloc, yloc, depth = model_gradient.shape
    parts = rows * cols
    block = depth // parts
    scaled = split_outside(depth_scale[:, :, None] * filter_z[None, :, :])
    pair_x, pair_y = split_outside(filter_x), split_outside(filter_y)
    arrived = []
    for index in range(params):
        outgoing = depth_pass(index, *scaled, model_gradient, parts, 8)
        arrived.append(
            lax.all_to_all(outgoing, AXES, split_axis=0, concat_axis=0, tiled=True)
        )
    output = None
    for index in range(params):
        field = arrived[index].reshape(rows, cols, yloc, block, xloc)
        field = second_pass(*pair_y, first_pass(*pair_x, field))
        field = field.reshape(parts, yloc, block, xloc)
        back = lax.all_to_all(field, AXES, split_axis=0, concat_axis=0, tiled=True)
        output = place(index, params, back, output, 8)
    return output


def plane_filter(incoming, filter_x, filter_y, rows, cols):
    xloc, yloc = incoming.shape[0], incoming.shape[1]
    matrix_x = filter_x.reshape(rows, xloc, rows, xloc)
    matrix_y = filter_y.reshape(cols, yloc, cols, yloc)
    partial_value = jnp.einsum(
        "ABRa,abRSz->ABbSz", matrix_x, incoming, precision=ACCURACY
    )
    return jnp.einsum(
        "CDSb,ABbSz->ACBDz", matrix_y, partial_value, precision=ACCURACY
    )


def plain_shards(model_gradient, filter_x, filter_y, filter_z, depth_scale):
    rows, cols = lax.axis_size("row"), lax.axis_size("col")
    params, xloc, yloc, depth = model_gradient.shape
    parts = rows * cols
    block = depth // parts
    arrived = []
    for index in range(params):
        scaled_filter = depth_scale[index][:, None] * filter_z
        column = jnp.einsum(
            "kz,abz->abk", scaled_filter, model_gradient[index], precision=ACCURACY
        )
        outgoing = column.reshape(xloc, yloc, parts, block)
        arrived.append(
            lax.all_to_all(outgoing, AXES, split_axis=2, concat_axis=2, tiled=True)
        )
    results = []
    for index in range(params):
        incoming = arrived[index].reshape(xloc, yloc, rows, cols, block)
        planes = plane_filter(incoming, filter_x, filter_y, rows, cols)
        planes = planes.reshape(parts, xloc, yloc, block)
        back = lax.all_to_all(planes, AXES, split_axis=0, concat_axis=3, tiled=True)
        results.append(back.reshape(xloc, yloc, depth))
    return jnp.stack(results)


def shards(model_gradient, filter_x, filter_y, filter_z, depth_scale):
    _, xloc, yloc, depth = model_gradient.shape
    block = depth // (lax.axis_size("row") * lax.axis_size("col"))
    aligned = block % 8 == 0 and xloc % 128 == 0 and yloc % 8 == 0
    chosen = kernel_shards if aligned else plain_shards
    return chosen(model_gradient, filter_x, filter_y, filter_z, depth_scale)


def solution(mesh):
    return jax.shard_map(
        shards,
        mesh=mesh,
        in_specs=(P(None, "row", "col", None), P(), P(), P(), P()),
        out_specs=P(None, "row", "col", None),
        check_vma=False,
    )
```

time: 1320 us -> 1180 us (0.89)
  blocking collectives: 547 us -> 0 us
  waiting for transfers between devices: 542 us -> 918 us
  Pallas kernels: 0 us -> 230 us
  matrix products: 140 us -> 0 us
  local copies, waits for them, and re-layouts: 87.5 us -> 0.01 us
  starting transfers between devices: 7.62 us -> 26.3 us
    all_to_all x1 -> x0, blocking collectives: 547 us -> none  [shards(): lax.all_to_all(planes, ('row', 'col'), split_axis=0, concat_axis=4, tiled...]
    all_to_all x1 -> x6, waiting for transfers between devices: 542 us -> 918 us  [the longest x3 465 us: kernel_shards(): back = lax.all_to_all(field, AXES, split_axis=0, concat_axis=0, tiled=True)]
    pallas_call x0 -> x12, Pallas kernels: none -> 230 us  [the longest x3 96.1 us: depth_pass(): pl.pallas_call(depth_kernel, grid=(yloc // tile,), in_specs=[pl.BlockSpec...]
    dot_general x3 -> x0, matrix products: 140 us -> none  [the longest x1 49.8 us: plane_filter(): jnp.einsum('ABRa,pabRSz->ABpbSz', matrix_x, incoming_part, precision=high...]
    reshape x5 -> x0, local copies, waits for them, and re-layouts: 61.3 us -> none  [the longest x2 42.1 us: shards(): return result.reshape(params, xloc, yloc, depth)]
    transpose x1 -> x0, local copies, waits for them, and re-layouts: 26.2 us -> none  [plane_filter(): jnp.einsum('CDSb,ABpbSz->ACpBDz', lateral_y_matrix, partial_value, precis...]
    all_to_all x1 -> x6, starting transfers between devices: 7.62 us -> 26.3 us  [the longest x3 15 us: kernel_shards(): lax.all_to_all(outgoing, AXES, split_axis=0, concat_axis=0, tiled=True)]
  transfers between devices with their start and end apart: 1 -> 6, of which waited for: 1 -> 6; matrix products, arithmetic and copies ran while one was open for 0% -> 0% of each run, Pallas kernels for 0% -> 16%
where the time goes in v1:
time: 1180 us
  waiting for transfers between devices  918 us (78%)
  Pallas kernels  230 us (19%)
  starting transfers between devices  26.3 us (2%)
    all_to_all x3, waiting for transfers between devices, kernel_shards(): back = lax.all_to_all(field, AXES, split_axis=0, concat_axis=0, tiled=True)  465 us
    all_to_all x3, waiting for transfers between devices, kernel_shards(): lax.all_to_all(outgoing, AXES, split_axis=0, concat_axis=0, tiled=True)  453 us
    pallas_call x3, Pallas kernels, depth_pass(): pl.pallas_call(depth_kernel, grid=(yloc // tile,), in_specs=[pl.BlockSpec...  96.1 us
    pallas_call x3, Pallas kernels, second_pass(): pl.pallas_call(second_kernel, grid=(rows,), in_specs=[whole, whole, spec]...  52.2 us
    pallas_call x3, Pallas kernels, first_pass(): pl.pallas_call(first_kernel, grid=(cols,), in_specs=[whole, whole, spec],...  51.1 us
    pallas_call x3, Pallas kernels, place(): pl.pallas_call(place_kernel, grid=(yloc // tile,), in_specs=[pl.BlockSpec...  30.9 us
  transfers between devices with their start and end apart: 6, of which 6 were waited for; matrix products, arithmetic and copies ran while one was open for 0% of the time, Pallas kernels for 16%

profile of v1, /device:TPU:0, one launch (start us, length us, event | category | flops | bytes accessed | tf_op | source)
XLA Modules:
  0.0 1179.0 jit_solution(420466932309976594)
XLA Ops:
  0.0 2.1 fusion.2
  2.1 32.0 %shard_map.61 = f32[32,64,8,128]{3,2,1,0:T(8,128)} custom-call(bf16[3,256,256]{2,1,0:T(8,128)(2,1)} %get-tuple-element.10.high_ref, bf16[3,256,256]{2,1,0:T(8,128)(2,1)} %get-tuple-element.9.low_ref, f32[3,128,64,256]{3,2,1,0:T(8,128)} %field_ref.5), custom_call_target="tpu_custom_call" | custom-call | flops 3221225472 | bytes 16777216 | tf_op jit(solution)/shard_map/pallas_call | solution.py:48
  34.1 7.5 all-to-all-start.4
  41.5 32.1 %shard_map.58 = f32[32,64,8,128]{3,2,1,0:T(8,128)} custom-call(bf16[3,256,256]{2,1,0:T(8,128)(2,1)} %get-tuple-element.10.high_ref, bf16[3,256,256]{2,1,0:T(8,128)(2,1)} %get-tuple-element.9.low_ref, f32[3,128,64,256]{3,2,1,0:T(8,128)} %field_ref.5), custom_call_target="tpu_custom_call" | custom-call | flops 3221225472 | bytes 16777216 | tf_op jit(solution)/shard_map/pallas_call | solution.py:48
  73.6 152.7 %all-to-all-done.4 = f32[32,64,8,128]{3,2,1,0:T(8,128)} async-done(((f32[32,64,8,128]{3,2,1,0:T(8,128)}), f32[32,64,8,128]{3,2,1,0:T(8,128)}, u32[]{:S(2)}, u32[]{:S(2)}) %all-to-all-start.4) | async-done | bytes 8388640 | tf_op jit(solution)/shard_map/all_to_all | solution.py:149
  226.3 3.7 all-to-all-start.2
  230.0 32.0 %shard_map.55 = f32[32,64,8,128]{3,2,1,0:T(8,128)} custom-call(bf16[3,256,256]{2,1,0:T(8,128)(2,1)} %get-tuple-element.10.high_ref, bf16[3,256,256]{2,1,0:T(8,128)(2,1)} %get-tuple-element.9.low_ref, f32[3,128,64,256]{3,2,1,0:T(8,128)} %field_ref.5), custom_call_target="tpu_custom_call" | custom-call | flops 3221225472 | bytes 16777216 | tf_op jit(solution)/shard_map/pallas_call | solution.py:48
  262.0 0.0 copy-start
  262.0 0.0 copy-start.1
  262.0 152.8 %all-to-all-done.2 = f32[32,64,8,128]{3,2,1,0:T(8,128)} async-done(((f32[32,64,8,128]{3,2,1,0:T(8,128)}), f32[32,64,8,128]{3,2,1,0:T(8,128)}, u32[]{:S(2)}, u32[]{:S(2)}) %all-to-all-start.2) | async-done | bytes 8388640 | tf_op jit(solution)/shard_map/all_to_all | solution.py:149
  414.8 3.9 all-to-all-start
  418.7 0.0 copy-done
  418.7 1.2 fusion.1
  419.9 0.0 copy-done.1
  419.9 1.1 fusion
  421.0 17.0 %shard_map.62.in_ref = f32[4,8,64,8,128]{4,3,2,1,0:T(8,128)} custom-call(bf16[512,512]{1,0:T(8,128)(2,1)} %get-tuple-element.6.high_ref, bf16[512,512]{1,0:T(8,128)(2,1)} %get-tuple-element.5.low_ref, f32[4,8,64,8,128]{4,3,2,1,0:T(8,128)} %bitcast.4.in_ref), custom_call_target="tpu_custom_call" | custom-call | flops 6442450944 | bytes 16777216 | tf_op jit(solution)/shard_map/pallas_call | solution.py:77
  438.0 17.4 %shard_map.63 = f32[4,8,64,8,128]{4,3,2,1,0:T(8,128)} custom-call(bf16[512,512]{1,0:T(8,128)(2,1)} %get-tuple-element.8.high_ref, bf16[512,512]{1,0:T(8,128)(2,1)} %get-tuple-element.7.low_ref, f32[4,8,64,8,128]{4,3,2,1,0:T(8,128)} %shard_map.62.in_ref), custom_call_target="tpu_custom_call" | custom-call | flops 6442450944 | bytes 16777216 | tf_op jit(solution)/shard_map/pallas_call | solution.py:104
  455.5 147.8 %all-to-all-done = f32[32,64,8,128]{3,2,1,0:T(8,128)} async-done(((f32[32,64,8,128]{3,2,1,0:T(8,128)}), f32[32,64,8,128]{3,2,1,0:T(8,128)}, u32[]{:S(2)}, u32[]{:S(2)}) %all-to-all-start) | async-done | bytes 8388640 | tf_op jit(solution)/shard_map/all_to_all | solution.py:149
  603.3 3.7 all-to-all-start.5
  607.0 17.1 %shard_map.59.in_ref = f32[4,8,64,8,128]{4,3,2,1,0:T(8,128)} custom-call(bf16[512,512]{1,0:T(8,128)(2,1)} %get-tuple-element.6.high_ref, bf16[512,512]{1,0:T(8,128)(2,1)} %get-tuple-element.5.low_ref, f32[4,8,64,8,128]{4,3,2,1,0:T(8,128)} %bitcast.2.in_ref), custom_call_target="tpu_custom_call" | custom-call | flops 6442450944 | bytes 16777216 | tf_op jit(solution)/shard_map/pallas_call | solution.py:77
  624.0 17.4 %shard_map.60 = f32[4,8,64,8,128]{4,3,2,1,0:T(8,128)} custom-call(bf16[512,512]{1,0:T(8,128)(2,1)} %get-tuple-element.8.high_ref, bf16[512,512]{1,0:T(8,128)(2,1)} %get-tuple-element.7.low_ref, f32[4,8,64,8,128]{4,3,2,1,0:T(8,128)} %shard_map.59.in_ref), custom_call_target="tpu_custom_call" | custom-call | flops 6442450944 | bytes 16777216 | tf_op jit(solution)/shard_map/pallas_call | solution.py:104
  641.4 150.4 %all-to-all-done.5.in_ref = f32[32,64,8,128]{3,2,1,0:T(8,128)} async-done(((f32[32,64,8,128]{3,2,1,0:T(8,128)}), f32[32,64,8,128]{3,2,1,0:T(8,128)}, u32[]{:S(2)}, u32[]{:S(2)}) %all-to-all-start.5) | async-done | bytes 8388640 | tf_op jit(solution)/shard_map/all_to_all | solution.py:156
  791.8 3.9 all-to-all-start.3
  795.7 17.1 %shard_map.56.in_ref = f32[4,8,64,8,128]{4,3,2,1,0:T(8,128)} custom-call(bf16[512,512]{1,0:T(8,128)(2,1)} %get-tuple-element.6.high_ref, bf16[512,512]{1,0:T(8,128)(2,1)} %get-tuple-element.5.low_ref, f32[4,8,64,8,128]{4,3,2,1,0:T(8,128)} %bitcast.in_ref), custom_call_target="tpu_custom_call" | custom-call | flops 6442450944 | bytes 16777216 | tf_op jit(solution)/shard_map/pallas_call | solution.py:77
  812.7 17.4 %shard_map.57 = f32[4,8,64,8,128]{4,3,2,1,0:T(8,128)} custom-call(bf16[512,512]{1,0:T(8,128)(2,1)} %get-tuple-element.8.high_ref, bf16[512,512]{1,0:T(8,128)(2,1)} %get-tuple-element.7.low_ref, f32[4,8,64,8,128]{4,3,2,1,0:T(8,128)} %shard_map.56.in_ref), custom_call_target="tpu_custom_call" | custom-call | flops 6442450944 | bytes 16777216 | tf_op jit(solution)/shard_map/pallas_call | solution.py:104
  830.2 150.1 %all-to-all-done.3.in_ref = f32[32,64,8,128]{3,2,1,0:T(8,128)} async-done(((f32[32,64,8,128]{3,2,1,0:T(8,128)}), f32[32,64,8,128]{3,2,1,0:T(8,128)}, u32[]{:S(2)}, u32[]{:S(2)}) %all-to-all-start.3) | async-done | bytes 8388640 | tf_op jit(solution)/shard_map/all_to_all | solution.py:156
  980.2 3.7 all-to-all-start.1
  983.9 10.3 shard_map.64.refs_0_
  994.2 10.3 shard_map.65.refs_0_
  1004.5 164.2 %all-to-all-done.1.in_ref = f32[32,64,8,128]{3,2,1,0:T(8,128)} async-done(((f32[32,64,8,128]{3,2,1,0:T(8,128)}), f32[32,64,8,128]{3,2,1,0:T(8,128)}, u32[]{:S(2)}, u32[]{:S(2)}) %all-to-all-start.1) | async-done | bytes 8388640 | tf_op jit(solution)/shard_map/all_to_all | solution.py:156
  1168.7 10.3 shard_map.66
Async XLA Ops:
  34.1 192.2 %all-to-all-start.4 = ((f32[32,64,8,128]{3,2,1,0:T(8,128)}), f32[32,64,8,128]{3,2,1,0:T(8,128)}, u32[]{:S(2)}, u32[]{:S(2)}) async-start(f32[32,64,8,128]{3,2,1,0:T(8,128)} %shard_map.61), calls=%async_computation.4 | async-start | bytes 16777216 | tf_op jit(solution)/shard_map/all_to_all | solution.py:149
  226.3 188.5 %all-to-all-start.2 = ((f32[32,64,8,128]{3,2,1,0:T(8,128)}), f32[32,64,8,128]{3,2,1,0:T(8,128)}, u32[]{:S(2)}, u32[]{:S(2)}) async-start(f32[32,64,8,128]{3,2,1,0:T(8,128)} %shard_map.58), calls=%async_computation.2 | async-start | bytes 16777216 | tf_op jit(solution)/shard_map/all_to_all | solution.py:149
  262.0 156.6 %copy-start = (f32[512,512]{1,0:T(8,128)S(1)}, f32[512,512]{1,0:T(8,128)}, u32[]{:S(2)}) copy-start(f32[512,512]{1,0:T(8,128)} %param.6) | copy-start | bytes 3145732
  262.0 157.8 %copy-start.1 = (f32[512,512]{1,0:T(8,128)S(1)}, f32[512,512]{1,0:T(8,128)}, u32[]{:S(2)}) copy-start(f32[512,512]{1,0:T(8,128)} %param.7) | copy-start | bytes 3145732
  414.8 188.5 %all-to-all-start = ((f32[32,64,8,128]{3,2,1,0:T(8,128)}), f32[32,64,8,128]{3,2,1,0:T(8,128)}, u32[]{:S(2)}, u32[]{:S(2)}) async-start(f32[32,64,8,128]{3,2,1,0:T(8,128)} %shard_map.55), calls=%async_computation | async-start | bytes 16777216 | tf_op jit(solution)/shard_map/all_to_all | solution.py:149
  603.3 188.5 %all-to-all-start.5 = ((f32[32,64,8,128]{3,2,1,0:T(8,128)}), f32[32,64,8,128]{3,2,1,0:T(8,128)}, u32[]{:S(2)}, u32[]{:S(2)}) async-start(f32[32,64,8,128]{3,2,1,0:T(8,128)} %bitcast.8), calls=%async_computation.5 | async-start | bytes 16777216 | tf_op jit(solution)/shard_map/all_to_all | solution.py:156
  791.8 188.5 %all-to-all-start.3 = ((f32[32,64,8,128]{3,2,1,0:T(8,128)}), f32[32,64,8,128]{3,2,1,0:T(8,128)}, u32[]{:S(2)}, u32[]{:S(2)}) async-start(f32[32,64,8,128]{3,2,1,0:T(8,128)} %bitcast.6), calls=%async_computation.3 | async-start | bytes 16777216 | tf_op jit(solution)/shard_map/all_to_all | solution.py:156
  980.2 188.5 %all-to-all-start.1 = ((f32[32,64,8,128]{3,2,1,0:T(8,128)}), f32[32,64,8,128]{3,2,1,0:T(8,128)}, u32[]{:S(2)}, u32[]{:S(2)}) async-start(f32[32,64,8,128]{3,2,1,0:T(8,128)} %bitcast.7), calls=%async_computation.1 | async-start | bytes 16777216 | tf_op jit(solution)/shard_map/all_to_all | solution.py:156
